TPU v7x, 256 devices: a whole 4x4x8 slice. The times are simulated.
256 devices in a mesh: span: 64 (over y, x, z_lo, core), head: 4 (over z_hi).
Axes of the slice: x: 4, y: 4, z: 8 (z_hi: 4, z_lo: 2; z = z_hi * 2 + z_lo), core: 2. Of those that a mesh axis runs over, the one named last changes fastest.
Arguments:
- decoder_states: bfloat16 [131072, 1024], P('span'), may hold values from -21 to 21
- encodings: bfloat16 [4096, 128, 1024], P('span', 'head'), may hold values from -21 to 21
- neighbor_table: int32 [2048, 2, 2], P('span'), may hold values from 0 to 63, as said below
- query_weight: bfloat16 [1024, 1024], P(None, 'head'), may hold values from -0.1875 to 0.1875
- key_weight: bfloat16 [1024, 1024], P(None, 'head'), may hold values from -0.1875 to 0.1875
- value_weight: bfloat16 [1024, 1024], P(None, 'head'), may hold values from -0.1875 to 0.1875
- out_weight: bfloat16 [1024, 1024], P('head'), may hold values from -0.1875 to 0.1875
Outputs:
- attended: bfloat16 [131072, 1024], P('span', 'head')
Inputs may be any that keep to these rules, and one draw needn't show every extreme that they name: neighbor_table[c, k, 0] is the database shard and neighbor_table[c, k, 1] the slot in that shard of neighbor k of span c; in each aligned block of 32 spans (the spans of one device along `span`) every shard is named by exactly one neighbor, and every slot of every shard is named exactly once in the whole table.
All inputs are finite; a program needn't handle non-finite values.
Results may differ from a plain program's by a relative error of at most 0.012.
The roundings to bfloat16 on the way count: a program that leaves them out, or rounds other values in their place, can miss the bound.
Values may be sent and summed in bfloat16 or wider, within the bound.
A program may use at most 128 MiB of HBM per device.

v0:
```python
import jax
import jax.numpy as jnp
from jax import lax
from jax.sharding import PartitionSpec as P

HEAD_DIM = 64
SPAN_LEN = 64
SEQ_LEN = 2048


def body(
    decoder_states, encodings, neighbor_table, query_weight, key_weight, value_weight, out_weight
):
    peer_count = lax.axis_size("span")
    column_rows = lax.all_to_all(out_weight, "head", split_axis=1, concat_axis=0, tiled=True)
    shard_ids = neighbor_table[:, :, 0].reshape(-1)
    slot_ids = neighbor_table[:, :, 1].reshape(-1)
    entries = shard_ids.shape[0]
    per_peer = entries // peer_count
    numbering = jnp.arange(entries, dtype=jnp.int32)
    same_before = (shard_ids[:, None] == shard_ids[None, :]) & (
        numbering[None, :] < numbering[:, None]
    )
    ranking = jnp.sum(same_before.astype(jnp.int32), axis=1)
    position = shard_ids * per_peer + ranking
    placed = position[None, :] == numbering[:, None]
    request = jnp.sum(jnp.where(placed, slot_ids[None, :], 0), axis=1)
    wanted = lax.all_to_all(request, "span", split_axis=0, concat_axis=0, tiled=True)
    selected = encodings[wanted]
    model_width = decoder_states.shape[1]
    group_cols = query_weight.shape[1]
    both_weights = jnp.concatenate([key_weight, value_weight], axis=1)
    arrived = lax.all_to_all(selected, "span", split_axis=0, concat_axis=0, tiled=True)
    block_in = lax.all_gather(arrived, "head", axis=1, tiled=True)
    flattened = block_in.reshape(-1, model_width)
    result = jnp.dot(flattened, both_weights, preferred_element_type=jnp.float32).astype(
        jnp.bfloat16
    )
    projected = result.reshape(block_in.shape[0], block_in.shape[1], 2 * group_cols)
    ordered = projected[position]
    span_count = neighbor_table.shape[0]
    neighbors = neighbor_table.shape[1]
    heads_here = group_cols // HEAD_DIM
    ordered = ordered.reshape(span_count, neighbors * projected.shape[1], 2 * group_cols)
    key_rows = ordered[:, :, :group_cols].reshape(span_count, -1, heads_here, HEAD_DIM)
    value_rows = ordered[:, :, group_cols:].reshape(span_count, -1, heads_here, HEAD_DIM)
    queries = jnp.dot(decoder_states, query_weight, preferred_element_type=jnp.float32).astype(
        jnp.bfloat16
    )
    sequences = decoder_states.shape[0] // SEQ_LEN
    offset = SPAN_LEN - 1
    queries = queries.reshape(sequences, SEQ_LEN, group_cols)
    shifted = jnp.concatenate(
        [queries[:, offset:], jnp.zeros((sequences, offset, group_cols), jnp.bfloat16)], axis=1
    )
    shifted = shifted.reshape(span_count, SPAN_LEN, heads_here, HEAD_DIM)
    inv_root = HEAD_DIM ** (-0.5)
    scores = (
        jnp.einsum("cqhd,ckhd->chqk", shifted, key_rows, preferred_element_type=jnp.float32)
        * inv_root
    )
    weights = jax.nn.softmax(scores, axis=-1).astype(jnp.bfloat16)
    context = jnp.einsum(
        "chqk,ckhd->cqhd", weights, value_rows, preferred_element_type=jnp.float32
    ).astype(jnp.bfloat16)
    context = context.reshape(sequences, SEQ_LEN, group_cols)
    context = jnp.concatenate(
        [jnp.zeros((sequences, offset, group_cols), jnp.bfloat16), context[:, : SEQ_LEN - offset]],
        axis=1,
    )
    context = context.reshape(-1, group_cols)
    summed = jnp.dot(
        lax.all_gather(context, "head", axis=1, tiled=True),
        column_rows,
        preferred_element_type=jnp.float32,
    )
    return summed.astype(jnp.bfloat16)


def solution(mesh):
    return jax.shard_map(
        body,
        mesh=mesh,
        in_specs=(
            P("span", None),
            P("span", "head", None),
            P("span", None, None),
            P(None, "head"),
            P(None, "head"),
            P(None, "head"),
            P("head", None),
        ),
        out_specs=P("span", "head"),
        check_vma=False,
    )
```

profile of v0, /device:TPU:33, one launch (start us, length us, event | category | flops | bytes accessed | tf_op | source)
XLA Modules:
  0.0 560.3 jit_solution(16839109739039627777)
XLA Ops:
  6.5 0.0 copy-start
  6.5 0.0 all-gather.4.cloned.1.call-start
  6.5 0.8 fusion.30
  7.3 0.1 copy.50
  7.4 0.1 reshape_squeeze.5
  7.5 0.2 convert_reduce_fusion
  7.7 0.1 copy.51
  7.8 0.1 broadcast_in_dim.14
  7.9 0.1 select_reduce_fusion
  8.0 0.1 copy.52
  8.1 15.8 %all_to_all.36 = s32[64,1,1]{2,1,0:T(1,128)S(1)} all-to-all(s32[64,1,1]{2,1,0:T(1,128)S(1)} %copy.52), channel_id=1, replica_groups=mesh['span'=64,'head'=4] {'span'}, dimensions={0} | all-to-all | bytes 512 | tf_op jit(solution)/shard_map/all_to_all | solution.py:28
  23.9 1.2 reduce
  25.1 4.9 gather_fusion
  30.1 56.3 %all_to_all.37 = bf16[64,32,1024]{2,1,0:T(8,128)(2,1)} all-to-all(bf16[64,32,1024]{2,1,0:T(8,128)(2,1)} %gather_fusion), channel_id=1, replica_groups=mesh['span'=64,'head'=4] {'span'}, dimensions={0} | all-to-all | bytes 8388608 | tf_op jit(solution)/shard_map/all_to_all | solution.py:33
  86.4 0.0 all-gather.4.cloned.1.call-update
  86.4 0.2 all-gather.6.cloned.1.call-start
  86.6 0.1 reshape_squeeze.6
  86.7 0.0 copy-done
  86.7 3.4 fusion.11
  90.2 0.0 copy-start.4
  90.2 0.2 slice.29
  90.4 1.0 concatenate.10
  91.5 3.3 reshape.100
  94.8 285.4 %all-gather.4.cloned.1.call-done = bf16[64,128,1024]{2,1,0:T(8,128)(2,1)} async-done(((bf16[64,32,1024]{2,1,0:T(8,128)(2,1)}), bf16[64,128,1024]{2,1,0:T(8,128)(2,1)}) %all-gather.4.cloned.1.call-update) | async-done | bytes 16777232 | tf_op jit(solution)/shard_map/all_gather | solution.py:34
  380.3 0.0 copy-done.4
  380.3 14.5 %convolution_convert_fusion = bf16[8192,512]{1,0:T(8,128)(2,1)} fusion(bf16[8192,1024]{1,0:T(8,128)(2,1)} %bitcast.54, bf16[1024,256]{1,0:T(8,128)(2,1)S(1)} %copy-done.4, bf16[1024,256]{1,0:T(8,128)(2,1)} %param.11), kind=kOutput, calls=%fused_computation.3 | convolution fusion | flops 8596226048 | bytes 26214400 | tf_op jit(solution)/shard_map/dot_general | solution.py:36
  394.8 8.9 %gather_fusion.1 = bf16[64,128,512]{2,1,0:T(8,128)(2,1)} fusion(bf16[64,128,512]{2,1,0:T(8,128)(2,1)} %bitcast.47, s32[1024]{0:T(1024)S(1)} %pad_clamp_fusion), kind=kCustom, calls=%fused_computation.1 | custom fusion | bytes 16777472 | tf_op jit(solution)/shard_map/gather | solution.py:40
  403.7 5.9 %fusion.29 = (bf16[32,256,256]{2,1,0:T(8,128)(2,1)}, bf16[32,256,256]{2,1,0:T(8,128)(2,1)}) fusion(bf16[32,256,512]{2,1,0:T(8,128)(2,1)} %bitcast.45), kind=kLoop, calls=%fused_computation.37 | loop fusion | bytes 16777216 | tf_op jit(solution)/shard_map/slice | solution.py:45
  409.6 6.4 %copy.61 = bf16[32,256,256]{1,2,0:T(8,128)(2,1)} copy(bf16[32,256,256]{2,1,0:T(8,128)(2,1)} %get-tuple-element.5) | data formatting | bytes 8388608
  416.0 3.4 fusion.12
  419.4 0.0 copy-start.2
  419.4 3.1 fusion.31
  422.6 0.1 copy-done.2
  422.6 6.4 %copy.60 = bf16[32,256,256]{1,2,0:T(8,128)(2,1)} copy(bf16[32,256,256]{2,1,0:T(8,128)(2,1)} %get-tuple-element.6) | data formatting | bytes 8388608
  429.0 22.4 %convert_bitcast_fusion = bf16[32,64,4,64]{1,3,2,0:T(8,128)(2,1)} fusion(bf16[32,256,4,64]{1,3,2,0:T(8,128)(2,1)} %bitcast.49, f32[32,4,64]{2,1,0:T(4,128)S(1)} %fusion.31, f32[32,4,64,256]{3,2,1,0:T(8,128)} %copy-done.2), kind=kOutput, calls=%fused_computation.17 | convolution fusion | flops 279453952 | bytes 13664256 | tf_op jit(solution)/shard_map/chqk,ckhd->cqhd/dot_general | solution.py:63
  451.4 2.9 copy.57
  454.4 0.0 copy-start.3
  454.4 2.4 reshape.102
  456.8 2.6 concatenate.11
  459.4 0.0 all-gather.6.cloned.1.call-update
  459.5 0.0 copy-done.3
  459.5 0.2 copy.58
  459.7 16.1 %all_to_all.38 = bf16[256,4,256]{0,2,1:T(8,128)(2,1)S(1)} all-to-all(bf16[256,4,256]{0,2,1:T(8,128)(2,1)S(1)} %bitcast.51), channel_id=1, replica_groups=mesh['span'=64,'head'=4] {'head'}, dimensions={1} | all-to-all | bytes 1048576 | tf_op jit(solution)/shard_map/all_to_all | solution.py:15
  475.8 0.2 copy.59
  476.0 72.9 %all-gather.6.cloned.1.call-done = bf16[1,2048,1024]{1,2,0:T(8,128)(2,1)} async-done(((bf16[1,2048,256]{1,2,0:T(8,128)(2,1)}), bf16[1,2048,1024]{1,2,0:T(8,128)(2,1)}) %all-gather.6.cloned.1.call-update) | async-done | bytes 4194320 | tf_op jit(solution)/shard_map/all_gather | solution.py:73
  548.9 0.0 copy-start.1
  548.9 4.5 fusion.8
  553.4 0.0 copy-done.1
  (5 shorter events, 0.0 us)
Async XLA Ops:
  6.5 80.2 %copy-start = (bf16[1024,256]{1,0:T(8,128)(2,1)S(1)}, bf16[1024,256]{1,0:T(8,128)(2,1)}, u32[]{:S(2)}) copy-start(bf16[1024,256]{1,0:T(8,128)(2,1)} %param.10) | copy-start | bytes 1572868
  6.5 373.7 %all-gather.4.cloned.1.call-start = ((), (), s32[]{:S(2)}) async-start(), calls=%async_computation.3 | async-start | bytes 20971520 | tf_op jit(solution)/shard_map/all_gather | solution.py:34
  86.4 462.5 %all-gather.6.cloned.1.call-start = ((), (), s32[]{:S(2)}) async-start(), calls=%async_computation.4 | async-start | bytes 5242880 | tf_op jit(solution)/shard_map/all_gather | solution.py:73
  90.2 290.1 %copy-start.4 = (bf16[1024,256]{1,0:T(8,128)(2,1)S(1)}, bf16[1024,256]{1,0:T(8,128)(2,1)}, u32[]{:S(2)}) copy-start(bf16[1024,256]{1,0:T(8,128)(2,1)} %param.12) | copy-start | bytes 1572868
  419.4 3.2 copy-start.2
  454.4 5.1 copy-start.3
  548.9 4.6 copy-start.1
Sparse Core Ops, SparseCore 0:
  86.5 293.6 all-gather.3
  459.6 89.2 all-gather.5
where the time goes:
time: 561 us; the launch traced here: 560 us
  waiting for transfers between devices  358 us (64%)
  blocking collectives  88.2 us (16%)
  matrix products  48.3 us (9%)
  local copies, waits for them, and re-layouts  47 us (8%)
  between operations  13.5 us (2%)
    all_gather x1, waiting for transfers between devices, body(): block_in = lax.all_gather(arrived, 'head', axis=1, tiled=True)  285 us
    all_gather x1, waiting for transfers between devices, body(): lax.all_gather(context, 'head', axis=1, tiled=True)  72.9 us
    all_to_all x1, blocking collectives, body(): lax.all_to_all(selected, 'span', split_axis=0, concat_axis=0, tiled=True)  56.3 us
    dot_general x1, matrix products, body(): jnp.einsum('chqk,ckhd->cqhd', weights, value_rows, preferred_element_type...  22.4 us
    all_to_all x1, blocking collectives, body(): lax.all_to_all(out_weight, 'head', split_axis=1, concat_axis=0, tiled=True)  16.1 us
    all_to_all x1, blocking collectives, body(): lax.all_to_all(request, 'span', split_axis=0, concat_axis=0, tiled=True)  15.8 us
    dot_general x1, matrix products, body(): jnp.dot(flattened, both_weights, preferred_element_type=jnp.float32)  14.5 us
    unnamed x13, local copies, waits for them, and re-layouts  13.1 us
  transfers between devices with their start and end apart: 2, of which 2 were waited for; matrix products, arithmetic and copies ran while one was open for 2% of the time, Pallas kernels for 0%

commit v1 on v0

--- a/solution.py
+++ b/solution.py
@@ -31,7 +31,9 @@
     group_cols = query_weight.shape[1]
     both_weights = jnp.concatenate([key_weight, value_weight], axis=1)
     arrived = lax.all_to_all(selected, "span", split_axis=0, concat_axis=0, tiled=True)
-    block_in = lax.all_gather(arrived, "head", axis=1, tiled=True)
+    block_in = jnp.concatenate(
+        lax.all_to_all(jnp.stack([arrived] * lax.axis_size("head")), "head", 0, 0), axis=1
+    )
     flattened = block_in.reshape(-1, model_width)
     result = jnp.dot(flattened, both_weights, preferred_element_type=jnp.float32).astype(
         jnp.bfloat16

time: 561 us -> 651 us (1.16)
  blocking collectives: 88.2 us -> 228 us
  waiting for transfers between devices: 358 us -> 291 us
  local copies, waits for them, and re-layouts: 47 us -> 58.9 us
  starting transfers between devices: 0.22 us -> 7.28 us
    all_gather x1 -> x0, waiting for transfers between devices: 285 us -> none  [body(): block_in = lax.all_gather(arrived, 'head', axis=1, tiled=True)]
    all_to_all x0 -> x1, waiting for transfers between devices: none -> 217 us  [body(): lax.all_to_all(jnp.stack([arrived] * lax.axis_size('head')), 'head', 0, 0)]
    all_to_all x1, blocking collectives: 16.1 us -> 156 us  [body(): lax.all_to_all(out_weight, 'head', split_axis=1, concat_axis=0, tiled=True)]
    all_to_all x0 -> x1, local copies, waits for them, and re-layouts: none -> 8.26 us  [body(): lax.all_to_all(jnp.stack([arrived] * lax.axis_size('head')), 'head', 0, 0)]
    all_to_all x0 -> x1, starting transfers between devices: none -> 7.28 us  [body(): lax.all_to_all(jnp.stack([arrived] * lax.axis_size('head')), 'head', 0, 0)]
    unnamed x13 -> x15, local copies, waits for them, and re-layouts: 13.1 us -> 13.2 us
  transfers between devices with their start and end apart: 2 -> 2, of which waited for: 2 -> 2; matrix products, arithmetic and copies ran while one was open for 2% -> 1% of each run, Pallas kernels for 0% -> 0%
where the time goes in v1:
time: 651 us; the launch traced here: 649 us
  waiting for transfers between devices  291 us (45%)
  blocking collectives  228 us (35%)
  local copies, waits for them, and re-layouts  58.9 us (9%)
  matrix products  45.8 us (7%)
  between operations  13.5 us (2%)
  starting transfers between devices  7.28 us (1%)
    all_to_all x1, waiting for transfers between devices, body(): lax.all_to_all(jnp.stack([arrived] * lax.axis_size('head')), 'head', 0, 0)  217 us
    all_to_all x1, blocking collectives, body(): lax.all_to_all(out_weight, 'head', split_axis=1, concat_axis=0, tiled=True)  156 us
    all_gather x1, waiting for transfers between devices, body(): lax.all_gather(context, 'head', axis=1, tiled=True)  73.6 us
    all_to_all x1, blocking collectives, body(): lax.all_to_all(selected, 'span', split_axis=0, concat_axis=0, tiled=True)  55.6 us
    dot_general x1, matrix products, body(): jnp.einsum('chqk,ckhd->cqhd', weights, value_rows, preferred_element_type...  22.4 us
    all_to_all x1, blocking collectives, body(): lax.all_to_all(request, 'span', split_axis=0, concat_axis=0, tiled=True)  15.8 us
    unnamed x15, local copies, waits for them, and re-layouts  13.2 us
  transfers between devices with their start and end apart: 2, of which 2 were waited for; matrix products, arithmetic and copies ran while one was open for 1% of the time, Pallas kernels for 0%

profile of v1, /device:TPU:33, one launch (start us, length us, event | category | flops | bytes accessed | tf_op | source)
XLA Modules:
  0.0 648.6 jit_solution(4953353238552204917)
XLA Ops:
  6.5 0.0 copy-start
  6.5 0.8 fusion.30
  7.3 0.1 copy.52
  7.4 0.1 reshape_squeeze.5
  7.5 0.2 convert_reduce_fusion
  7.7 0.1 copy.53
  7.8 0.1 broadcast_in_dim.14
  7.9 0.1 select_reduce_fusion
  8.0 0.1 copy.54
  8.1 15.8 %all_to_all.41 = s32[64,1,1]{2,1,0:T(1,128)S(1)} all-to-all(s32[64,1,1]{2,1,0:T(1,128)S(1)} %copy.54), channel_id=1, replica_groups=mesh['span'=64,'head'=4] {'span'}, dimensions={0} | all-to-all | bytes 512 | tf_op jit(solution)/shard_map/all_to_all | solution.py:28
  23.9 1.2 reduce
  25.1 4.9 gather_fusion
  30.1 55.6 %all_to_all.42 = bf16[64,32,1024]{2,1,0:T(8,128)(2,1)S(1)} all-to-all(bf16[64,32,1024]{2,1,0:T(8,128)(2,1)} %gather_fusion), channel_id=1, replica_groups=mesh['span'=64,'head'=4] {'span'}, dimensions={0} | all-to-all | bytes 8388608 | tf_op jit(solution)/shard_map/all_to_all | solution.py:33
  85.6 5.9 stack.2
  91.6 7.3 %all-to-all-start.2 = ((bf16[4,64,32,1024]{3,2,1,0:T(8,128)(2,1)}), bf16[4,64,32,1024]{3,2,1,0:T(8,128)(2,1)}, u32[]{:S(2)}, u32[]{:S(2)}) async-start(bf16[4,64,32,1024]{3,2,1,0:T(8,128)(2,1)} %stack.2), calls=%async_computation.2 | async-start | bytes 33554432 | tf_op jit(solution)/shard_map/all_to_all | solution.py:35
  98.9 0.0 all-gather.3.cloned.1.call-start
  98.9 0.1 reshape_squeeze.6
  99.0 0.0 copy-done
  99.0 3.4 fusion.11
  102.4 0.2 slice.29
  102.7 0.1 concatenate.10
  102.8 1.8 reshape.102
  104.6 0.0 copy-start.5
  104.6 217.2 %all-to-all-done.2 = bf16[4,64,32,1024]{3,2,1,0:T(8,128)(2,1)} async-done(((bf16[4,64,32,1024]{3,2,1,0:T(8,128)(2,1)}), bf16[4,64,32,1024]{3,2,1,0:T(8,128)(2,1)}, u32[]{:S(2)}, u32[]{:S(2)}) %all-to-all-start.2) | async-done | bytes 16777248 | tf_op jit(solution)/shard_map/all_to_all | solution.py:35
  321.8 8.3 %copy.55 = bf16[4,64,32,1024]{3,2,0,1:T(8,128)(2,1)S(1)} copy(bf16[4,64,32,1024]{3,2,1,0:T(8,128)(2,1)} %all-to-all-done.2) | data formatting | bytes 33554432 | tf_op jit(solution)/shard_map/all_to_all | solution.py:35
  330.1 0.0 copy-done.5
  330.1 12.0 %convolution_convert_fusion = bf16[8192,512]{1,0:T(8,128)(2,1)} fusion(bf16[8192,1024]{1,0:T(8,128)(2,1)S(1)} %bitcast.49, bf16[1024,256]{1,0:T(8,128)(2,1)S(1)} %copy-done.5, bf16[1024,256]{1,0:T(8,128)(2,1)} %param.11), kind=kOutput, calls=%fused_computation.3 | convolution fusion | flops 8596226048 | bytes 26214400 | tf_op jit(solution)/shard_map/dot_general | solution.py:38
  342.1 8.9 %gather_fusion.1 = bf16[64,128,512]{2,1,0:T(8,128)(2,1)} fusion(bf16[64,128,512]{2,1,0:T(8,128)(2,1)} %bitcast.50, s32[1024]{0:T(1024)S(1)} %pad_clamp_fusion), kind=kCustom, calls=%fused_computation.1 | custom fusion | bytes 16777472 | tf_op jit(solution)/shard_map/gather | solution.py:42
  351.1 5.9 fusion.29
  357.0 0.0 copy-start.3
  357.0 6.6 %copy.64 = bf16[32,256,256]{1,2,0:T(8,128)(2,1)} copy(bf16[32,256,256]{2,1,0:T(8,128)(2,1)} %get-tuple-element.5) | data formatting | bytes 8388608
  363.5 0.0 copy-done.3
  363.5 3.4 fusion.12
  367.0 0.0 copy-start.2
  367.0 3.1 fusion.31
  370.1 0.1 copy-done.2
  370.2 6.4 copy.63
  376.6 22.4 %convert_bitcast_fusion = bf16[32,64,4,64]{1,3,2,0:T(8,128)(2,1)} fusion(bf16[32,256,4,64]{1,3,2,0:T(8,128)(2,1)} %bitcast.52, f32[32,4,64]{2,1,0:T(4,128)S(1)} %fusion.31, f32[32,4,64,256]{3,2,1,0:T(8,128)} %copy-done.2), kind=kOutput, calls=%fused_computation.17 | convolution fusion | flops 279453952 | bytes 13664256 | tf_op jit(solution)/shard_map/chqk,ckhd->cqhd/dot_general | solution.py:65
  399.0 2.9 copy.60
  401.9 0.0 copy-start.4
  401.9 2.4 reshape.104
  404.3 2.6 concatenate.11
  407.0 0.0 all-gather.3.cloned.1.call-update
  407.0 0.0 copy-done.4
  407.0 0.2 copy.61
  407.2 156.2 %all_to_all.43 = bf16[256,4,256]{0,2,1:T(8,128)(2,1)S(1)} all-to-all(bf16[256,4,256]{0,2,1:T(8,128)(2,1)S(1)} %bitcast.54), channel_id=1, replica_groups=mesh['span'=64,'head'=4] {'head'}, dimensions={1} | all-to-all | bytes 1048576 | tf_op jit(solution)/shard_map/all_to_all | solution.py:15
  563.4 0.2 copy.62
  563.6 73.6 %all-gather.3.cloned.1.call-done = bf16[1,2048,1024]{1,2,0:T(8,128)(2,1)} async-done(((bf16[1,2048,256]{1,2,0:T(8,128)(2,1)}), bf16[1,2048,1024]{1,2,0:T(8,128)(2,1)}) %all-gather.3.cloned.1.call-update) | async-done | bytes 4194320 | tf_op jit(solution)/shard_map/all_gather | solution.py:75
  637.2 0.0 copy-start.1
  637.2 4.6 fusion.8
  641.8 0.0 copy-done.1
  (5 shorter events, 0.0 us)
Async XLA Ops:
  6.5 92.4 %copy-start = (bf16[1024,256]{1,0:T(8,128)(2,1)S(1)}, bf16[1024,256]{1,0:T(8,128)(2,1)}, u32[]{:S(2)}) copy-start(bf16[1024,256]{1,0:T(8,128)(2,1)} %param.10) | copy-start | bytes 1572868
  91.6 230.2 %all-to-all-start.2 = ((bf16[4,64,32,1024]{3,2,1,0:T(8,128)(2,1)}), bf16[4,64,32,1024]{3,2,1,0:T(8,128)(2,1)}, u32[]{:S(2)}, u32[]{:S(2)}) async-start(bf16[4,64,32,1024]{3,2,1,0:T(8,128)(2,1)} %stack.2), calls=%async_computation.2 | async-start | bytes 33554432 | tf_op jit(solution)/shard_map/all_to_all | solution.py:35
  98.9 538.3 %all-gather.3.cloned.1.call-start = ((), (), s32[]{:S(2)}) async-start(), calls=%async_computation.4 | async-start | bytes 5242880 | tf_op jit(solution)/shard_map/all_gather | solution.py:75
  104.6 225.5 %copy-start.5 = (bf16[1024,256]{1,0:T(8,128)(2,1)S(1)}, bf16[1024,256]{1,0:T(8,128)(2,1)}, u32[]{:S(2)}) copy-start(bf16[1024,256]{1,0:T(8,128)(2,1)} %param.12) | copy-start | bytes 1572868
  357.0 6.6 %copy-start.3 = (bf16[32,64,4,64]{3,2,1,0:T(4,128)(2,1)S(1)}, bf16[32,64,4,64]{3,2,1,0:T(4,128)(2,1)}, u32[]{:S(2)}) copy-start(bf16[32,64,4,64]{3,2,1,0:T(4,128)(2,1)} %reshape.102) | copy-start | bytes 3145732
  367.0 3.2 copy-start.2
  401.9 5.1 copy-start.4
  637.2 4.6 copy-start.1
Sparse Core Ops, SparseCore 0:
  407.1 230.0 all-gather.2
